TPU v7x, 128 devices: a whole 4x4x4 slice. The times are simulated.
128 devices in a mesh: genes: 64 (over z, y, x_hi, core), cols: 2 (over x_lo).
Axes of the slice: x: 4 (x_hi: 2, x_lo: 2; x = x_hi * 2 + x_lo), y: 4, z: 4, core: 2. Of those that a mesh axis runs over, the one named last changes fastest.
Arguments:
- expression: float32 [384, 40960], P(None, ('genes', 'cols')), may hold values from -200 to 200
- resample: int32 [384], replicated, may hold values from 0 to 383
- labels: int32 [40960, 300], P(('genes', 'cols')), may hold values from 0 to 1, as said below
- ref_kim: float32 [40960], P(('genes', 'cols')), may hold values from 0 to 1
Outputs:
- connectivity: float32 [40960, 300], P(('genes', 'cols'))
- preservation: float32 [2, 300], replicated
Inputs may be any that keep to these rules, and one draw needn't show every extreme that they name: `labels`: each row holds exactly one 1; every module has 32 or more genes.
All inputs are finite; a program needn't handle non-finite values.
Results may differ from a plain program's by a relative error of at most 0.0031.
Values may be sent and summed in bfloat16 or wider, within the bound.
A program may use at most 64 MiB of HBM per device.

v0:
```python
import math
import jax
import jax.numpy as jnp
from jax import lax
from jax.sharding import Mesh
from jax.sharding import PartitionSpec as P

G = 40960
GENES = ("genes_0", "genes_1", "genes_2", "genes_3")
GENES_COLS = ("genes_0", "genes_1", "genes_2", "genes_3", "cols")


def in_order(blocks, dim):
    lengths = list(blocks.shape[1:])
    lengths[dim] *= blocks.shape[0]
    return jnp.moveaxis(blocks, 0, dim).reshape(lengths)


def sent_to_all(x, axis):
    copies = jnp.broadcast_to(x, (lax.axis_size(axis), *x.shape))
    return lax.all_to_all(copies, axis, split_axis=0, concat_axis=0, tiled=True)


def gathered_copies(x, axis, dim):
    return in_order(sent_to_all(x, axis), dim)


def split_up(x, dim, count):
    before, after = (x.shape[:dim], x.shape[dim + 1 :])
    return jnp.moveaxis(x.reshape(*before, count, -1, *after), dim, 0)


def sum_at_owner(x, axis, dim):
    count = lax.axis_size(axis)
    blocks = lax.all_to_all(split_up(x, dim, count), axis, 0, 0, tiled=True)
    return jnp.sum(blocks.astype(jnp.float32), axis=0)


def one_axis_at_a_time(x, axes):
    for axis in axes:
        x = lax.psum(x, axis)
    return x


def standardize(expression, resample):
    boot = jnp.take(expression, resample, axis=0)
    centered = boot - jnp.mean(boot, axis=0, keepdims=True)
    total = jnp.sum(centered * centered, axis=0, keepdims=True)
    return (centered * lax.rsqrt(total + 1e-06)).astype(jnp.bfloat16)


def local_sums(connectivity, labels, ref_kim):
    member = labels.astype(jnp.float32)
    kim = jnp.sum(connectivity * member, axis=1)
    rowsum = jnp.sum(connectivity, axis=1)
    stacked = jnp.stack(
        [kim, kim * kim, ref_kim, ref_kim * ref_kim, kim * ref_kim, rowsum, jnp.ones_like(kim)],
        axis=1,
    )
    return jnp.dot(
        member.T, stacked, precision=lax.Precision.HIGHEST, preferred_element_type=jnp.float32
    )


def preserve(sums, total_genes):
    counts = sums[:, 6]
    mean_x = sums[:, 0] / (counts * counts)
    var_x = jnp.maximum(sums[:, 1] / (counts * counts * counts) - mean_x * mean_x, 0.0001)
    mean_y = sums[:, 2] / counts
    var_y = jnp.maximum(sums[:, 3] / counts - mean_y * mean_y, 0.01)
    cross = sums[:, 4] / (counts * counts) - mean_x * mean_y
    between = (sums[:, 5] - sums[:, 0]) / (counts * (total_genes - counts))
    density = (mean_x - between) * jnp.sqrt(counts / var_x)
    linked = cross * jnp.sqrt(counts / (var_x * var_y))
    return jnp.stack([density, linked], axis=0)


def tile_term(row_block, column_block, column_ids, module_count):
    scores = lax.dot_general(
        row_block, column_block, (((0,), (0,)), ((), ())), preferred_element_type=jnp.float32
    )
    squares = scores * scores
    adjacency = (squares * squares * squares).astype(jnp.bfloat16)
    member_block = (
        column_ids[:, None] == jnp.arange(module_count, dtype=jnp.int32)[None, :]
    ).astype(jnp.bfloat16)
    return jnp.dot(adjacency, member_block, preferred_element_type=jnp.float32)


def add_tiles(carried, row_block, piece, every_ids, shard_width, module_count):
    span_width = piece.shape[1]
    column_step = shard_width * math.gcd(span_width // shard_width, 8)
    steps_total = span_width // column_step

    def one_step(step_index, accumulated):
        columns = lax.dynamic_slice_in_dim(piece, step_index * column_step, column_step, 1)
        column_ids = lax.dynamic_slice_in_dim(every_ids, step_index * column_step, column_step, 0)
        return accumulated + tile_term(row_block, columns, column_ids, module_count)

    return lax.fori_loop(0, steps_total, one_step, carried)


def local(expression, resample, labels, ref_kim):
    scaled = standardize(expression, resample)
    module_count = labels.shape[1]
    shard_width = scaled.shape[1]
    module_ids = jnp.sum(labels * jnp.arange(module_count, dtype=jnp.int32)[None, :], axis=1)
    row_block = gathered_copies(scaled, "cols", 1)
    panel_ids = gathered_copies(module_ids, GENES, 0)
    initial = jnp.zeros((row_block.shape[1], module_count), jnp.float32)
    partial_value = add_tiles(
        initial,
        row_block,
        lax.all_gather(scaled, GENES, axis=1, tiled=True),
        panel_ids,
        shard_width,
        module_count,
    )
    connectivity = sum_at_owner(partial_value.astype(jnp.bfloat16), "cols", 0)
    sums = one_axis_at_a_time(local_sums(connectivity, labels, ref_kim), GENES_COLS)
    return (connectivity, preserve(sums, G))


def solution(mesh):
    torus = Mesh(
        mesh.devices.reshape(4, 4, 2, 2, mesh.shape["cols"]),
        ("genes_0", "genes_1", "genes_2", "genes_3", "cols"),
    )
    placed = (P(None, GENES_COLS), P(), P(GENES_COLS, None), P(GENES_COLS))
    return jax.shard_map(
        local, mesh=torus, in_specs=placed, out_specs=(P(GENES_COLS, None), P()), check_vma=False
    )
```

profile of v0, /device:TPU:2, one launch (start us, length us, event | category | flops | bytes accessed | tf_op | source)
XLA Modules:
  0.0 233.6 jit_solution(9748620751659558973)
XLA Ops:
  7.2 0.0 copy-start
  7.2 0.0 all-gather.2.cloned.1.call-start
  7.2 0.7 compare_select_fusion
  8.0 0.7 compare_and_fusion
  8.6 1.3 copy.21
  9.9 1.7 gather_fusion
  11.7 0.2 copy.22
  11.9 0.2 select_reduce_fusion
  12.0 0.2 multiply_reduce_fusion
  12.3 0.9 multiply_convert_fusion
  13.1 0.0 all-gather.2.cloned.1.call-update
  13.2 0.0 copy-done
  13.2 0.1 multiply_reduce_fusion.2
  13.2 0.1 broadcast_in_dim.35
  13.3 20.1 %all_to_all.16 = s32[64,1,320]{2,1,0:T(1,128)S(1)} all-to-all(s32[64,1,320]{2,1,0:T(1,128)S(1)} %broadcast_in_dim.35), channel_id=1, replica_groups=mesh['genes_0'=4,'genes_1'=4,'genes_2'=2,'genes_3'=2,'cols'=2] {'genes_0..., dimensions={0} | all-to-all | bytes 163840 | tf_op jit(solution)/shard_map/all_to_all | solution.py:21
  33.4 1.8 broadcast_in_dim.34
  35.1 4.9 %all-to-all-start = ((bf16[2,384,320]{1,2,0:T(8,128)(2,1)}), bf16[2,384,320]{1,2,0:T(8,128)(2,1)S(1)}, u32[]{:S(2)}, u32[]{:S(2)}) async-start(bf16[2,384,320]{1,2,0:T(8,128)(2,1)} %broadcast_in_dim.34), calls=%async_computation | async-start | bytes 983040 | tf_op jit(solution)/shard_map/all_to_all | solution.py:21
  40.0 0.2 reduce.1
  40.3 0.1 reshape.235
  40.4 6.0 %all-to-all-done = bf16[2,384,320]{1,2,0:T(8,128)(2,1)S(1)} async-done(((bf16[2,384,320]{1,2,0:T(8,128)(2,1)}), bf16[2,384,320]{1,2,0:T(8,128)(2,1)S(1)}, u32[]{:S(2)}, u32[]{:S(2)}) %all-to-all-start) | async-done | bytes 491552 | tf_op jit(solution)/shard_map/all_to_all | solution.py:21
  46.4 0.3 copy.24
  46.6 69.9 %all-gather.2.cloned.1.call-done = bf16[384,20480]{0,1:T(8,128)(2,1)} async-done(((bf16[384,320]{0,1:T(8,128)(2,1)}), bf16[384,20480]{0,1:T(8,128)(2,1)}) %all-gather.2.cloned.1.call-update) | async-done | bytes 15728656 | tf_op jit(solution)/shard_map/all_gather | solution.py:114
  116.5 0.0 copy-start.2
  116.5 43.6 %while.14 = (s32[]{:T(128)}, f32[640,300]{0,1:T(8,128)S(1)}, bf16[384,20480]{0,1:T(8,128)(2,1)}, bf16[384,640]{1,0:T(8,128)(2,1)S(1)}, s32[20480]{0:T(1024)S(1)}...) while((s32[]{:T(128)}, f32[640,300]{0,1:T(8,128)S(1)}, bf16[384,20480]{0,1:T(8,128)(2,1)}, ...), condition=%wide.region_4.5_spmd.clone, body=%wide.region_3.4_spmd.clone.sunk | while | flops 2249036800 | bytes 4024477 | solution.py:100
  116.5 0.1 dynamic_slice.25
  116.6 5.3 %fusion.32 = f32[640,300]{0,1:T(8,128)S(1)} fusion(s32[2560]{0:T(1024)S(1)} %dynamic_slice.25, bf16[384,640]{1,0:T(8,128)(2,1)S(1)} %get-tuple-element.204, bf16[384,20480]{0,1:T(8,128)(2,1)} %get-tuple-element.203, s32[]{:T(128)S(6)} %select_n.27, f32[640,300]{0,1:T(8,128)S(1)} %get-tuple-element.193, pred[]{:T(512)S(6)} %compare.3), kind=kOutput, calls=%fused_computation.7.clone.1 | convolution fusion | flops 2249036800 | bytes 4003845 | tf_op jit(solution)/shard_map/while/body/eval_jaxpr/dot_general | solution.py:87
  122.0 0.1 dynamic_slice.25
  122.1 5.3 %fusion.32 = f32[640,300]{0,1:T(8,128)S(1)} fusion(s32[2560]{0:T(1024)S(1)} %dynamic_slice.25, bf16[384,640]{1,0:T(8,128)(2,1)S(1)} %get-tuple-element.204, bf16[384,20480]{0,1:T(8,128)(2,1)} %get-tuple-element.203, s32[]{:T(128)S(6)} %select_n.27, f32[640,300]{0,1:T(8,128)S(1)} %get-tuple-element.193, pred[]{:T(512)S(6)} %compare.3), kind=kOutput, calls=%fused_computation.7.clone.1 | convolution fusion | flops 2249036800 | bytes 4003845 | tf_op jit(solution)/shard_map/while/body/eval_jaxpr/dot_general | solution.py:87
  127.4 0.1 dynamic_slice.25
  127.5 5.3 %fusion.32 = f32[640,300]{0,1:T(8,128)S(1)} fusion(s32[2560]{0:T(1024)S(1)} %dynamic_slice.25, bf16[384,640]{1,0:T(8,128)(2,1)S(1)} %get-tuple-element.204, bf16[384,20480]{0,1:T(8,128)(2,1)} %get-tuple-element.203, s32[]{:T(128)S(6)} %select_n.27, f32[640,300]{0,1:T(8,128)S(1)} %get-tuple-element.193, pred[]{:T(512)S(6)} %compare.3), kind=kOutput, calls=%fused_computation.7.clone.1 | convolution fusion | flops 2249036800 | bytes 4003845 | tf_op jit(solution)/shard_map/while/body/eval_jaxpr/dot_general | solution.py:87
  132.9 0.1 dynamic_slice.25
  133.0 5.3 %fusion.32 = f32[640,300]{0,1:T(8,128)S(1)} fusion(s32[2560]{0:T(1024)S(1)} %dynamic_slice.25, bf16[384,640]{1,0:T(8,128)(2,1)S(1)} %get-tuple-element.204, bf16[384,20480]{0,1:T(8,128)(2,1)} %get-tuple-element.203, s32[]{:T(128)S(6)} %select_n.27, f32[640,300]{0,1:T(8,128)S(1)} %get-tuple-element.193, pred[]{:T(512)S(6)} %compare.3), kind=kOutput, calls=%fused_computation.7.clone.1 | convolution fusion | flops 2249036800 | bytes 4003845 | tf_op jit(solution)/shard_map/while/body/eval_jaxpr/dot_general | solution.py:87
  138.3 0.1 dynamic_slice.25
  138.4 5.3 %fusion.32 = f32[640,300]{0,1:T(8,128)S(1)} fusion(s32[2560]{0:T(1024)S(1)} %dynamic_slice.25, bf16[384,640]{1,0:T(8,128)(2,1)S(1)} %get-tuple-element.204, bf16[384,20480]{0,1:T(8,128)(2,1)} %get-tuple-element.203, s32[]{:T(128)S(6)} %select_n.27, f32[640,300]{0,1:T(8,128)S(1)} %get-tuple-element.193, pred[]{:T(512)S(6)} %compare.3), kind=kOutput, calls=%fused_computation.7.clone.1 | convolution fusion | flops 2249036800 | bytes 4003845 | tf_op jit(solution)/shard_map/while/body/eval_jaxpr/dot_general | solution.py:87
  143.8 0.1 dynamic_slice.25
  143.9 5.3 %fusion.32 = f32[640,300]{0,1:T(8,128)S(1)} fusion(s32[2560]{0:T(1024)S(1)} %dynamic_slice.25, bf16[384,640]{1,0:T(8,128)(2,1)S(1)} %get-tuple-element.204, bf16[384,20480]{0,1:T(8,128)(2,1)} %get-tuple-element.203, s32[]{:T(128)S(6)} %select_n.27, f32[640,300]{0,1:T(8,128)S(1)} %get-tuple-element.193, pred[]{:T(512)S(6)} %compare.3), kind=kOutput, calls=%fused_computation.7.clone.1 | convolution fusion | flops 2249036800 | bytes 4003845 | tf_op jit(solution)/shard_map/while/body/eval_jaxpr/dot_general | solution.py:87
  149.2 0.1 dynamic_slice.25
  149.3 5.3 %fusion.32 = f32[640,300]{0,1:T(8,128)S(1)} fusion(s32[2560]{0:T(1024)S(1)} %dynamic_slice.25, bf16[384,640]{1,0:T(8,128)(2,1)S(1)} %get-tuple-element.204, bf16[384,20480]{0,1:T(8,128)(2,1)} %get-tuple-element.203, s32[]{:T(128)S(6)} %select_n.27, f32[640,300]{0,1:T(8,128)S(1)} %get-tuple-element.193, pred[]{:T(512)S(6)} %compare.3), kind=kOutput, calls=%fused_computation.7.clone.1 | convolution fusion | flops 2249036800 | bytes 4003845 | tf_op jit(solution)/shard_map/while/body/eval_jaxpr/dot_general | solution.py:87
  154.7 0.1 dynamic_slice.25
  154.8 5.3 %fusion.32 = f32[640,300]{0,1:T(8,128)S(1)} fusion(s32[2560]{0:T(1024)S(1)} %dynamic_slice.25, bf16[384,640]{1,0:T(8,128)(2,1)S(1)} %get-tuple-element.204, bf16[384,20480]{0,1:T(8,128)(2,1)} %get-tuple-element.203, s32[]{:T(128)S(6)} %select_n.27, f32[640,300]{0,1:T(8,128)S(1)} %get-tuple-element.193, pred[]{:T(512)S(6)} %compare.3), kind=kOutput, calls=%fused_computation.7.clone.1 | convolution fusion | flops 2249036800 | bytes 4003845 | tf_op jit(solution)/shard_map/while/body/eval_jaxpr/dot_general | solution.py:87
  160.2 0.4 reshape.236
  160.6 0.8 copy.25
  161.5 5.0 %all-to-all-start.2 = ((bf16[2,320,300]{1,2,0:T(8,128)(2,1)}), bf16[2,320,300]{1,2,0:T(8,128)(2,1)S(1)}, u32[]{:S(2)}, u32[]{:S(2)}) async-start(bf16[2,320,300]{1,2,0:T(8,128)(2,1)} %copy.25), calls=%async_computation.2 | async-start | bytes 933888 | tf_op jit(solution)/shard_map/all_to_all | solution.py:35
  166.4 0.0 copy-done.2
  166.4 6.3 %all-to-all-done.2 = bf16[2,320,300]{1,2,0:T(8,128)(2,1)S(1)} async-done(((bf16[2,320,300]{1,2,0:T(8,128)(2,1)}), bf16[2,320,300]{1,2,0:T(8,128)(2,1)S(1)}, u32[]{:S(2)}, u32[]{:S(2)}) %all-to-all-start.2) | async-done | bytes 384032 | tf_op jit(solution)/shard_map/all_to_all | solution.py:35
  172.7 0.2 convert_reduce_fusion
  172.9 0.0 copy-start.1
  172.9 0.1 multiply_reduce_fusion.1
  173.1 0.4 convolution_bitcast_fusion
  173.6 17.1 %psum.35 = f32[300,7]{0,1:T(8,128)S(1)} all-reduce(f32[300,7]{0,1:T(8,128)S(1)} %convolution_bitcast_fusion), channel_id=1, replica_groups=mesh['genes_0'=4,'genes_1'=4,'genes_2'=2,'genes_3'=2,'cols'=2] {'genes_0'}, use_global_device_ids=true, to_apply=%region_8.9 | all-reduce | flops 2100 | bytes 16800 | tf_op jit(solution)/shard_map/psum | solution.py:41
  190.7 14.9 %psum.36 = f32[300,7]{0,1:T(8,128)S(1)} all-reduce(f32[300,7]{0,1:T(8,128)S(1)} %psum.35), channel_id=1, replica_groups=mesh['genes_0'=4,'genes_1'=4,'genes_2'=2,'genes_3'=2,'cols'=2] {'genes_1'}, use_global_device_ids=true, to_apply=%region_9.10 | all-reduce | flops 2100 | bytes 16800 | tf_op jit(solution)/shard_map/psum | solution.py:41
  205.6 8.2 %psum.37 = f32[300,7]{0,1:T(8,128)S(1)} all-reduce(f32[300,7]{0,1:T(8,128)S(1)} %psum.36), channel_id=1, replica_groups=mesh['genes_0'=4,'genes_1'=4,'genes_2'=2,'genes_3'=2,'cols'=2] {'genes_2'}, use_global_device_ids=true, to_apply=%region_10.11 | all-reduce | flops 2100 | bytes 16800 | tf_op jit(solution)/shard_map/psum | solution.py:41
  213.8 3.3 %psum.38 = f32[300,7]{0,1:T(8,128)S(1)} all-reduce(f32[300,7]{0,1:T(8,128)S(1)} %psum.37), channel_id=1, replica_groups=mesh['genes_0'=4,'genes_1'=4,'genes_2'=2,'genes_3'=2,'cols'=2] {'genes_3'}, use_global_device_ids=true, to_apply=%region_11.12 | all-reduce | flops 2100 | bytes 16800 | tf_op jit(solution)/shard_map/psum | solution.py:41
  217.0 9.1 %psum.39 = f32[300,7]{0,1:T(8,128)S(1)} all-reduce(f32[300,7]{0,1:T(8,128)S(1)} %psum.38), channel_id=1, replica_groups=mesh['genes_0'=4,'genes_1'=4,'genes_2'=2,'genes_3'=2,'cols'=2] {'cols'}, use_global_device_ids=true, to_apply=%region_12.13 | all-reduce | flops 2100 | bytes 16800 | tf_op jit(solution)/shard_map/psum | solution.py:41
  226.2 0.6 pad_maximum_fusion
  226.8 0.0 copy-done.1
  (16 shorter events, 0.2 us)
Async XLA Ops:
  7.2 6.0 %copy-start = (s32[320,300]{0,1:T(8,128)S(1)}, s32[320,300]{0,1:T(8,128)}, u32[]{:S(2)}) copy-start(s32[320,300]{0,1:T(8,128)} %param.8) | copy-start | bytes 1152004
  7.2 109.3 %all-gather.2.cloned.1.call-start = ((), (), s32[]{:S(2)}) async-start(), calls=%async_computation.3 | async-start | bytes 15974400 | tf_op jit(solution)/shard_map/all_gather | solution.py:114
  35.1 11.2 %all-to-all-start = ((bf16[2,384,320]{1,2,0:T(8,128)(2,1)}), bf16[2,384,320]{1,2,0:T(8,128)(2,1)S(1)}, u32[]{:S(2)}, u32[]{:S(2)}) async-start(bf16[2,384,320]{1,2,0:T(8,128)(2,1)} %broadcast_in_dim.34), calls=%async_computation | async-start | bytes 983040 | tf_op jit(solution)/shard_map/all_to_all | solution.py:21
  116.5 49.9 %copy-start.2 = (f32[320]{0:T(512)S(1)}, f32[320]{0:T(512)}, u32[]{:S(2)}) copy-start(f32[320]{0:T(512)} %param.9) | copy-start | bytes 3844
  161.5 11.2 %all-to-all-start.2 = ((bf16[2,320,300]{1,2,0:T(8,128)(2,1)}), bf16[2,320,300]{1,2,0:T(8,128)(2,1)S(1)}, u32[]{:S(2)}, u32[]{:S(2)}) async-start(bf16[2,320,300]{1,2,0:T(8,128)(2,1)} %copy.25), calls=%async_computation.2 | async-start | bytes 933888 | tf_op jit(solution)/shard_map/all_to_all | solution.py:35
  172.9 53.8 %copy-start.1 = (f32[320,300]{0,1:T(8,128)}, f32[320,300]{0,1:T(8,128)S(1)}, u32[]{:S(2)}) copy-start(f32[320,300]{0,1:T(8,128)S(1)} %get-tuple-element.136) | copy-start | bytes 1152004
Sparse Core Ops, SparseCore 0:
  13.3 103.1 all-gather.1
where the time goes:
time: 234 us
  waiting for transfers between devices  82.2 us (35%)
  blocking collectives  72.6 us (31%)
  matrix products  43.2 us (18%)
  between operations  14.2 us (6%)
  starting transfers between devices  9.89 us (4%)
  local copies, waits for them, and re-layouts  7.35 us (3%)
  other arithmetic  4.01 us (2%)
    all_gather x1, waiting for transfers between devices, local(): lax.all_gather(scaled, GENES, axis=1, tiled=True)  69.9 us
    psum x5, blocking collectives, one_axis_at_a_time(): x = lax.psum(x, axis)  52.5 us
    dot_general x8, matrix products, tile_term(): return jnp.dot(adjacency, member_block, preferred_element_type=jnp.float32)  42.8 us
    all_to_all x1, blocking collectives, sent_to_all(): return lax.all_to_all(copies, axis, split_axis=0, concat_axis=0, tiled=True)  20.1 us
    all_to_all x1, waiting for transfers between devices, sum_at_owner(): blocks = lax.all_to_all(split_up(x, dim, count), axis, 0, 0, tiled=True)  6.29 us
    all_to_all x1, waiting for transfers between devices, sent_to_all(): return lax.all_to_all(copies, axis, split_axis=0, concat_axis=0, tiled=True)  5.99 us
    all_to_all x1, starting transfers between devices, sum_at_owner(): blocks = lax.all_to_all(split_up(x, dim, count), axis, 0, 0, tiled=True)  4.95 us
    all_to_all x1, starting transfers between devices, sent_to_all(): return lax.all_to_all(copies, axis, split_axis=0, concat_axis=0, tiled=True)  4.9 us
  transfers between devices with their start and end apart: 3, of which 3 were waited for; matrix products, arithmetic and copies ran while one was open for 1% of the time, Pallas kernels for 0%

commit v1 on v0

--- a/solution.py
+++ b/solution.py
@@ -38,7 +38,7 @@
 
 def one_axis_at_a_time(x, axes):
     for axis in axes:
-        x = lax.psum(x, axis)
+        x = jax.lax.all_gather(x, axis_name=axis).sum(axis=0)
     return x
 
 

time: 234 us -> 220 us (0.940)
  blocking collectives: 72.6 us -> 56.6 us
    psum x5 -> x0, blocking collectives: 52.5 us -> none  [one_axis_at_a_time(): x = lax.psum(x, axis)]
    all_gather x0 -> x5, blocking collectives: none -> 36.5 us  [one_axis_at_a_time(): x = jax.lax.all_gather(x, axis_name=axis).sum(axis=0)]
where the time goes in v1:
time: 220 us; the launch traced here: 218 us
  waiting for transfers between devices  82.2 us (37%)
  blocking collectives  56.6 us (26%)
  matrix products  43.2 us (20%)
  between operations  14.2 us (6%)
  starting transfers between devices  9.89 us (4%)
  local copies, waits for them, and re-layouts  7.35 us (3%)
  other arithmetic  4.05 us (2%)
    all_gather x1, waiting for transfers between devices, local(): lax.all_gather(scaled, GENES, axis=1, tiled=True)  69.9 us
    dot_general x8, matrix products, tile_term(): return jnp.dot(adjacency, member_block, preferred_element_type=jnp.float32)  42.8 us
    all_gather x5, blocking collectives, one_axis_at_a_time(): x = jax.lax.all_gather(x, axis_name=axis).sum(axis=0)  36.5 us
    all_to_all x1, blocking collectives, sent_to_all(): return lax.all_to_all(copies, axis, split_axis=0, concat_axis=0, tiled=True)  20.1 us
    all_to_all x1, waiting for transfers between devices, sum_at_owner(): blocks = lax.all_to_all(split_up(x, dim, count), axis, 0, 0, tiled=True)  6.29 us
    all_to_all x1, waiting for transfers between devices, sent_to_all(): return lax.all_to_all(copies, axis, split_axis=0, concat_axis=0, tiled=True)  5.99 us
    all_to_all x1, starting transfers between devices, sum_at_owner(): blocks = lax.all_to_all(split_up(x, dim, count), axis, 0, 0, tiled=True)  4.95 us
    all_to_all x1, starting transfers between devices, sent_to_all(): return lax.all_to_all(copies, axis, split_axis=0, concat_axis=0, tiled=True)  4.9 us
  transfers between devices with their start and end apart: 3, of which 3 were waited for; matrix products, arithmetic and copies ran while one was open for 1% of the time, Pallas kernels for 0%

profile of v1, /device:TPU:2, one launch (start us, length us, event | category | flops | bytes accessed | tf_op | source)
XLA Modules:
  0.0 217.6 jit_solution(1173046854202709068)
XLA Ops:
  7.2 0.0 copy-start
  7.2 0.0 all-gather.12.cloned.1.call-start
  7.2 0.7 compare_select_fusion
  8.0 0.7 compare_and_fusion
  8.6 1.3 copy.21
  9.9 1.7 gather_fusion
  11.7 0.2 copy.22
  11.9 0.2 select_reduce_fusion
  12.0 0.2 multiply_reduce_fusion
  12.3 0.9 multiply_convert_fusion
  13.1 0.0 all-gather.12.cloned.1.call-update
  13.2 0.0 copy-done
  13.2 0.1 multiply_reduce_fusion.2
  13.2 0.1 broadcast_in_dim.35
  13.3 20.1 %all_to_all.16 = s32[64,1,320]{2,1,0:T(1,128)S(1)} all-to-all(s32[64,1,320]{2,1,0:T(1,128)S(1)} %broadcast_in_dim.35), channel_id=1, replica_groups=mesh['genes_0'=4,'genes_1'=4,'genes_2'=2,'genes_3'=2,'cols'=2] {'genes_0..., dimensions={0} | all-to-all | bytes 163840 | tf_op jit(solution)/shard_map/all_to_all | solution.py:21
  33.4 1.8 broadcast_in_dim.34
  35.1 4.9 %all-to-all-start = ((bf16[2,384,320]{1,2,0:T(8,128)(2,1)}), bf16[2,384,320]{1,2,0:T(8,128)(2,1)S(1)}, u32[]{:S(2)}, u32[]{:S(2)}) async-start(bf16[2,384,320]{1,2,0:T(8,128)(2,1)} %broadcast_in_dim.34), calls=%async_computation | async-start | bytes 983040 | tf_op jit(solution)/shard_map/all_to_all | solution.py:21
  40.0 0.2 reduce.6
  40.3 0.1 reshape.235
  40.4 6.0 %all-to-all-done = bf16[2,384,320]{1,2,0:T(8,128)(2,1)S(1)} async-done(((bf16[2,384,320]{1,2,0:T(8,128)(2,1)}), bf16[2,384,320]{1,2,0:T(8,128)(2,1)S(1)}, u32[]{:S(2)}, u32[]{:S(2)}) %all-to-all-start) | async-done | bytes 491552 | tf_op jit(solution)/shard_map/all_to_all | solution.py:21
  46.4 0.3 copy.24
  46.6 69.9 %all-gather.12.cloned.1.call-done = bf16[384,20480]{0,1:T(8,128)(2,1)} async-done(((bf16[384,320]{0,1:T(8,128)(2,1)}), bf16[384,20480]{0,1:T(8,128)(2,1)}) %all-gather.12.cloned.1.call-update) | async-done | bytes 15728656 | tf_op jit(solution)/shard_map/all_gather | solution.py:114
  116.5 0.0 copy-start.2
  116.5 43.6 %while.14 = (s32[]{:T(128)}, f32[640,300]{0,1:T(8,128)S(1)}, bf16[384,20480]{0,1:T(8,128)(2,1)}, bf16[384,640]{1,0:T(8,128)(2,1)S(1)}, s32[20480]{0:T(1024)S(1)}...) while((s32[]{:T(128)}, f32[640,300]{0,1:T(8,128)S(1)}, bf16[384,20480]{0,1:T(8,128)(2,1)}, ...), condition=%wide.region_4.5_spmd.clone, body=%wide.region_3.4_spmd.clone.sunk | while | flops 2249036800 | bytes 4024477 | solution.py:100
  116.5 0.1 dynamic_slice.25
  116.6 5.3 %fusion.32 = f32[640,300]{0,1:T(8,128)S(1)} fusion(s32[2560]{0:T(1024)S(1)} %dynamic_slice.25, bf16[384,640]{1,0:T(8,128)(2,1)S(1)} %get-tuple-element.204, bf16[384,20480]{0,1:T(8,128)(2,1)} %get-tuple-element.203, s32[]{:T(128)S(6)} %select_n.27, f32[640,300]{0,1:T(8,128)S(1)} %get-tuple-element.193, pred[]{:T(512)S(6)} %compare.3), kind=kOutput, calls=%fused_computation.7.clone.1 | convolution fusion | flops 2249036800 | bytes 4003845 | tf_op jit(solution)/shard_map/while/body/eval_jaxpr/dot_general | solution.py:87
  122.0 0.1 dynamic_slice.25
  122.1 5.3 %fusion.32 = f32[640,300]{0,1:T(8,128)S(1)} fusion(s32[2560]{0:T(1024)S(1)} %dynamic_slice.25, bf16[384,640]{1,0:T(8,128)(2,1)S(1)} %get-tuple-element.204, bf16[384,20480]{0,1:T(8,128)(2,1)} %get-tuple-element.203, s32[]{:T(128)S(6)} %select_n.27, f32[640,300]{0,1:T(8,128)S(1)} %get-tuple-element.193, pred[]{:T(512)S(6)} %compare.3), kind=kOutput, calls=%fused_computation.7.clone.1 | convolution fusion | flops 2249036800 | bytes 4003845 | tf_op jit(solution)/shard_map/while/body/eval_jaxpr/dot_general | solution.py:87
  127.4 0.1 dynamic_slice.25
  127.5 5.3 %fusion.32 = f32[640,300]{0,1:T(8,128)S(1)} fusion(s32[2560]{0:T(1024)S(1)} %dynamic_slice.25, bf16[384,640]{1,0:T(8,128)(2,1)S(1)} %get-tuple-element.204, bf16[384,20480]{0,1:T(8,128)(2,1)} %get-tuple-element.203, s32[]{:T(128)S(6)} %select_n.27, f32[640,300]{0,1:T(8,128)S(1)} %get-tuple-element.193, pred[]{:T(512)S(6)} %compare.3), kind=kOutput, calls=%fused_computation.7.clone.1 | convolution fusion | flops 2249036800 | bytes 4003845 | tf_op jit(solution)/shard_map/while/body/eval_jaxpr/dot_general | solution.py:87
  132.9 0.1 dynamic_slice.25
  133.0 5.3 %fusion.32 = f32[640,300]{0,1:T(8,128)S(1)} fusion(s32[2560]{0:T(1024)S(1)} %dynamic_slice.25, bf16[384,640]{1,0:T(8,128)(2,1)S(1)} %get-tuple-element.204, bf16[384,20480]{0,1:T(8,128)(2,1)} %get-tuple-element.203, s32[]{:T(128)S(6)} %select_n.27, f32[640,300]{0,1:T(8,128)S(1)} %get-tuple-element.193, pred[]{:T(512)S(6)} %compare.3), kind=kOutput, calls=%fused_computation.7.clone.1 | convolution fusion | flops 2249036800 | bytes 4003845 | tf_op jit(solution)/shard_map/while/body/eval_jaxpr/dot_general | solution.py:87
  138.3 0.1 dynamic_slice.25
  138.4 5.3 %fusion.32 = f32[640,300]{0,1:T(8,128)S(1)} fusion(s32[2560]{0:T(1024)S(1)} %dynamic_slice.25, bf16[384,640]{1,0:T(8,128)(2,1)S(1)} %get-tuple-element.204, bf16[384,20480]{0,1:T(8,128)(2,1)} %get-tuple-element.203, s32[]{:T(128)S(6)} %select_n.27, f32[640,300]{0,1:T(8,128)S(1)} %get-tuple-element.193, pred[]{:T(512)S(6)} %compare.3), kind=kOutput, calls=%fused_computation.7.clone.1 | convolution fusion | flops 2249036800 | bytes 4003845 | tf_op jit(solution)/shard_map/while/body/eval_jaxpr/dot_general | solution.py:87
  143.8 0.1 dynamic_slice.25
  143.9 5.3 %fusion.32 = f32[640,300]{0,1:T(8,128)S(1)} fusion(s32[2560]{0:T(1024)S(1)} %dynamic_slice.25, bf16[384,640]{1,0:T(8,128)(2,1)S(1)} %get-tuple-element.204, bf16[384,20480]{0,1:T(8,128)(2,1)} %get-tuple-element.203, s32[]{:T(128)S(6)} %select_n.27, f32[640,300]{0,1:T(8,128)S(1)} %get-tuple-element.193, pred[]{:T(512)S(6)} %compare.3), kind=kOutput, calls=%fused_computation.7.clone.1 | convolution fusion | flops 2249036800 | bytes 4003845 | tf_op jit(solution)/shard_map/while/body/eval_jaxpr/dot_general | solution.py:87
  149.2 0.1 dynamic_slice.25
  149.3 5.3 %fusion.32 = f32[640,300]{0,1:T(8,128)S(1)} fusion(s32[2560]{0:T(1024)S(1)} %dynamic_slice.25, bf16[384,640]{1,0:T(8,128)(2,1)S(1)} %get-tuple-element.204, bf16[384,20480]{0,1:T(8,128)(2,1)} %get-tuple-element.203, s32[]{:T(128)S(6)} %select_n.27, f32[640,300]{0,1:T(8,128)S(1)} %get-tuple-element.193, pred[]{:T(512)S(6)} %compare.3), kind=kOutput, calls=%fused_computation.7.clone.1 | convolution fusion | flops 2249036800 | bytes 4003845 | tf_op jit(solution)/shard_map/while/body/eval_jaxpr/dot_general | solution.py:87
  154.7 0.1 dynamic_slice.25
  154.8 5.3 %fusion.32 = f32[640,300]{0,1:T(8,128)S(1)} fusion(s32[2560]{0:T(1024)S(1)} %dynamic_slice.25, bf16[384,640]{1,0:T(8,128)(2,1)S(1)} %get-tuple-element.204, bf16[384,20480]{0,1:T(8,128)(2,1)} %get-tuple-element.203, s32[]{:T(128)S(6)} %select_n.27, f32[640,300]{0,1:T(8,128)S(1)} %get-tuple-element.193, pred[]{:T(512)S(6)} %compare.3), kind=kOutput, calls=%fused_computation.7.clone.1 | convolution fusion | flops 2249036800 | bytes 4003845 | tf_op jit(solution)/shard_map/while/body/eval_jaxpr/dot_general | solution.py:87
  160.2 0.4 reshape.236
  160.6 0.8 copy.25
  161.5 5.0 %all-to-all-start.2 = ((bf16[2,320,300]{1,2,0:T(8,128)(2,1)}), bf16[2,320,300]{1,2,0:T(8,128)(2,1)S(1)}, u32[]{:S(2)}, u32[]{:S(2)}) async-start(bf16[2,320,300]{1,2,0:T(8,128)(2,1)} %copy.25), calls=%async_computation.2 | async-start | bytes 933888 | tf_op jit(solution)/shard_map/all_to_all | solution.py:35
  166.4 0.0 copy-done.2
  166.4 6.3 %all-to-all-done.2 = bf16[2,320,300]{1,2,0:T(8,128)(2,1)S(1)} async-done(((bf16[2,320,300]{1,2,0:T(8,128)(2,1)}), bf16[2,320,300]{1,2,0:T(8,128)(2,1)S(1)}, u32[]{:S(2)}, u32[]{:S(2)}) %all-to-all-start.2) | async-done | bytes 384032 | tf_op jit(solution)/shard_map/all_to_all | solution.py:35
  172.7 0.2 convert_reduce_fusion
  172.9 0.0 copy-start.1
  172.9 0.1 multiply_reduce_fusion.1
  173.1 0.4 convolution_bitcast_fusion
  173.6 12.5 %all-gather.5 = f32[4,300,7]{1,2,0:T(8,128)S(1)} all-gather(f32[1,300,7]{1,2,0:T(8,128)S(1)} %convolution_bitcast_fusion), channel_id=2, replica_groups=mesh['genes_0'=4,'genes_1'=4,'genes_2'=2,'genes_3'=2,'cols'=2] {'genes_0'}, dimensions={0}, use_global_device_ids=true | all-gather | bytes 42000 | tf_op jit(solution)/shard_map/all_gather | solution.py:41
  186.0 11.9 %all-gather.6 = f32[4,300,7]{1,2,0:T(8,128)S(1)} all-gather(f32[1,300,7]{1,2,0:T(8,128)S(1)} %bitcast.89), channel_id=3, replica_groups=mesh['genes_0'=4,'genes_1'=4,'genes_2'=2,'genes_3'=2,'cols'=2] {'genes_1'}, dimensions={0}, use_global_device_ids=true | all-gather | bytes 42000 | tf_op jit(solution)/shard_map/all_gather | solution.py:41
  198.0 5.9 %all-gather.7 = f32[2,300,7]{1,2,0:T(8,128)S(1)} all-gather(f32[1,300,7]{1,2,0:T(8,128)S(1)} %bitcast.88), channel_id=4, replica_groups=mesh['genes_0'=4,'genes_1'=4,'genes_2'=2,'genes_3'=2,'cols'=2] {'genes_2'}, dimensions={0}, use_global_device_ids=true | all-gather | bytes 25200 | tf_op jit(solution)/shard_map/all_gather | solution.py:41
  203.9 1.8 all-gather.8
  205.7 4.4 %all-gather.9 = f32[2,300,7]{1,2,0:T(8,128)S(1)} all-gather(f32[1,300,7]{1,2,0:T(8,128)S(1)} %bitcast.87), channel_id=6, replica_groups=mesh['genes_0'=4,'genes_1'=4,'genes_2'=2,'genes_3'=2,'cols'=2] {'cols'}, dimensions={0}, use_global_device_ids=true | all-gather | bytes 25200 | tf_op jit(solution)/shard_map/all_gather | solution.py:41
  210.2 0.6 pad_maximum_fusion
  210.8 0.0 copy-done.1
  (21 shorter events, 0.2 us)
Async XLA Ops:
  7.2 6.0 %copy-start = (s32[320,300]{0,1:T(8,128)S(1)}, s32[320,300]{0,1:T(8,128)}, u32[]{:S(2)}) copy-start(s32[320,300]{0,1:T(8,128)} %param.8) | copy-start | bytes 1152004
  7.2 109.3 %all-gather.12.cloned.1.call-start = ((), (), s32[]{:S(2)}) async-start(), calls=%async_computation.3 | async-start | bytes 15974400 | tf_op jit(solution)/shard_map/all_gather | solution.py:114
  35.1 11.2 %all-to-all-start = ((bf16[2,384,320]{1,2,0:T(8,128)(2,1)}), bf16[2,384,320]{1,2,0:T(8,128)(2,1)S(1)}, u32[]{:S(2)}, u32[]{:S(2)}) async-start(bf16[2,384,320]{1,2,0:T(8,128)(2,1)} %broadcast_in_dim.34), calls=%async_computation | async-start | bytes 983040 | tf_op jit(solution)/shard_map/all_to_all | solution.py:21
  116.5 49.9 %copy-start.2 = (f32[320]{0:T(512)S(1)}, f32[320]{0:T(512)}, u32[]{:S(2)}) copy-start(f32[320]{0:T(512)} %param.9) | copy-start | bytes 3844
  161.5 11.2 %all-to-all-start.2 = ((bf16[2,320,300]{1,2,0:T(8,128)(2,1)}), bf16[2,320,300]{1,2,0:T(8,128)(2,1)S(1)}, u32[]{:S(2)}, u32[]{:S(2)}) async-start(bf16[2,320,300]{1,2,0:T(8,128)(2,1)} %copy.25), calls=%async_computation.2 | async-start | bytes 933888 | tf_op jit(solution)/shard_map/all_to_all | solution.py:35
  172.9 37.8 %copy-start.1 = (f32[320,300]{0,1:T(8,128)}, f32[320,300]{0,1:T(8,128)S(1)}, u32[]{:S(2)}) copy-start(f32[320,300]{0,1:T(8,128)S(1)} %get-tuple-element.136) | copy-start | bytes 1152004
Sparse Core Ops, SparseCore 0:
  13.3 103.1 all-gather.11
